TPU v7x, 32 devices: a whole 2x2x4 slice. The times are simulated.
32 devices in a mesh: narrow: 4 (over x, core), wide: 8 (over z, y).
Axes of the slice: x: 2, y: 2, z: 4, core: 2. Of those that a mesh axis runs over, the one named last changes fastest.
Arguments:
- block_ids: int32 [512, 4], P(('narrow', 'wide')), may hold values from 0 to 511, as said below
- incidence: int32 [512, 4, 128, 128], P(('narrow', 'wide')), may hold values from 0 to 1
- costs: int32 [512, 128], P(('narrow', 'wide')), may hold values from 16 to 80
- start_mult: float32 [512, 128], replicated, may hold values from 0.25 to 4
- upper: float32 [1], replicated, may hold values from 65536 to 131072
Outputs:
- multipliers: float32 [512, 128], replicated
- primal_mean: float32 [512, 128], P(('narrow', 'wide'))
Inputs may be any that keep to these rules, and one draw needn't show every extreme that they name: `block_ids`: the 4 row blocks listed for one tile are distinct.
All inputs are finite; a program needn't handle non-finite values.
Results may differ from a plain program's by a relative error of at most 0.0003.
Values sent between devices are 32-bit elements; how exact they have to be, the bound alone decides.
A program may use at most 64 MiB of HBM per device.

v0:
```python
import jax
import jax.numpy as jnp
from jax import lax
from jax.sharding import PartitionSpec as P

BLK = 128
K = 4
ITERS = 3


def local(block_ids, incidence, costs, start_mult, upper):
    hi = lax.Precision.HIGHEST
    tiles_here = block_ids.shape[0]
    blocks = start_mult.shape[0]
    incf = incidence.astype(jnp.float32)
    costf = costs.astype(jnp.float32)
    onehot = (
        block_ids.reshape(tiles_here * K, 1) == jnp.arange(blocks, dtype=jnp.int32)[None, :]
    ).astype(jnp.float32)
    count_narrow = lax.axis_size("narrow")
    count_wide = lax.axis_size("wide")
    share_rows = blocks // lax.axis_size(("narrow", "wide"))
    share_start = lax.axis_index(("narrow", "wide")) * share_rows
    mult = start_mult
    primal_mean = jnp.zeros(costs.shape, jnp.float32)
    for step in range(ITERS):
        u_tile = jnp.take(mult, block_ids, axis=0)
        reduced = costf - jnp.einsum("tkrc,tkr->tc", incf, u_tile, precision=hi)
        primal = 1.0 / (1.0 + jnp.exp(reduced / 8.0))
        local_soft = jnp.sum(-8.0 * jax.nn.softplus(-reduced / 8.0))
        if step == 0:
            primal_mean = primal
        else:
            primal_mean = 0.3 * primal + 0.7 * primal_mean
        part = jnp.einsum("tkrc,tc->tkr", incf, primal_mean, precision=hi).reshape(
            tiles_here * K, BLK
        )
        row_part = jnp.dot(onehot.T, part, precision=hi, preferred_element_type=jnp.float32)
        outgoing = row_part.reshape(count_narrow, count_wide, share_rows, BLK)
        incoming = lax.all_to_all(
            lax.all_to_all(outgoing, "narrow", split_axis=0, concat_axis=0, tiled=True),
            "wide",
            split_axis=1,
            concat_axis=1,
            tiled=True,
        )
        cover_share = jnp.sum(jnp.sum(incoming, axis=0), axis=0)
        mult_share = lax.dynamic_slice_in_dim(mult, share_start, share_rows, 0)
        slope = 1.0 - cover_share
        norm, mult_total, late_sum = lax.psum(
            (jnp.sum(slope * slope), jnp.sum(mult_share), local_soft), ("narrow", "wide")
        )
        value = mult_total + late_sum
        size = (upper[0] - value) / (norm + 1e-06)
        new_share = jnp.maximum(0.0, mult_share + size * slope)
        mult = lax.all_gather(new_share, ("narrow", "wide"), axis=0, tiled=True)
    return (mult, primal_mean)


def solution(mesh):
    in_specs = (
        P(("narrow", "wide"), None),
        P(("narrow", "wide"), None, None, None),
        P(("narrow", "wide"), None),
        P(),
        P(),
    )
    out_specs = (P(), P(("narrow", "wide"), None))
    return jax.shard_map(local, mesh=mesh, in_specs=in_specs, out_specs=out_specs, check_vma=False)
```

profile of v0, /device:TPU:0, one launch (start us, length us, event | category | flops | bytes accessed | tf_op | source)
XLA Modules:
  0.0 426.2 jit_solution(1178383881923371404)
XLA Ops:
  0.6 0.7 compare_and_fusion
  1.3 0.7 compare_select_fusion.3
  2.0 0.8 copy.23
  2.8 0.1 copy.21
  3.0 0.1 reshape.82
  3.1 0.1 eq.41
  3.2 1.5 gather_fusion
  4.7 0.1 broadcast_select_fusion.2
  4.8 4.1 fusion.10
  8.9 0.6 fusion.25
  9.6 3.4 fusion.8
  12.9 0.3 fusion.16
  13.3 10.0 %all_to_all.30 = f32[4,8,16,128]{3,2,1,0:T(8,128)S(1)} all-to-all(f32[4,8,16,128]{3,2,1,0:T(8,128)S(1)} %fusion.16), channel_id=1, replica_groups=mesh['narrow'=4,'wide'=8] {'narrow'}, dimensions={0} | all-to-all | bytes 524288 | tf_op jit(solution)/shard_map/all_to_all | solution.py:41
  23.3 0.7 copy.24
  24.1 5.8 %all-to-all-start.1 = ((f32[4,8,16,128]{3,2,0,1:T(8,128)}), f32[4,8,16,128]{3,2,0,1:T(8,128)S(1)}, u32[]{:S(2)}, u32[]{:S(2)}) async-start(f32[4,8,16,128]{3,2,0,1:T(8,128)} %copy.24), calls=%async_computation.1 | async-start | bytes 524288 | tf_op jit(solution)/shard_map/all_to_all | solution.py:40
  29.9 1.4 dynamic-slice_reduce_fusion.2
  32.6 5.8 %all-to-all-done.1 = f32[4,8,16,128]{3,2,0,1:T(8,128)S(1)} async-done(((f32[4,8,16,128]{3,2,0,1:T(8,128)}), f32[4,8,16,128]{3,2,0,1:T(8,128)S(1)}, u32[]{:S(2)}, u32[]{:S(2)}) %all-to-all-start.1) | async-done | bytes 262176 | tf_op jit(solution)/shard_map/all_to_all | solution.py:40
  38.5 0.6 multiply_reduce_fusion.2
  39.7 39.0 %all-reduce.2 = (f32[]{:T(128)}, f32[]{:T(128)}) all-reduce(f32[]{:T(128)S(6)} %add.95, f32[]{:T(128)} %multiply_reduce_fusion.2), channel_id=1, replica_groups=mesh['narrow'=4,'wide'=8] {'narrow','wide'}, use_global_device_ids=true, to_apply=%region_1.2 | all-reduce | flops 2 | bytes 16 | tf_op jit(solution)/shard_map/psum | solution.py:50
  80.1 0.7 add_maximum_fusion.2
  80.8 67.3 %all_gather.9 = f32[512,128]{1,0:T(8,128)S(1)} all-gather(f32[16,128]{1,0:T(8,128)S(1)} %add_maximum_fusion.2), channel_id=1, replica_groups=mesh['narrow'=4,'wide'=8] {'narrow','wide'}, dimensions={0}, use_global_device_ids=true | all-gather | bytes 270336 | tf_op jit(solution)/shard_map/all_gather | solution.py:56
  148.1 0.6 gather_fusion.1
  148.8 4.1 fusion.6
  152.9 0.6 fusion.27
  153.5 3.4 fusion.4
  156.9 0.3 fusion.14
  157.3 8.4 %all_to_all.31 = f32[4,8,16,128]{3,2,1,0:T(8,128)S(1)} all-to-all(f32[4,8,16,128]{3,2,1,0:T(8,128)S(1)} %fusion.14), channel_id=1, replica_groups=mesh['narrow'=4,'wide'=8] {'narrow'}, dimensions={0} | all-to-all | bytes 524288 | tf_op jit(solution)/shard_map/all_to_all | solution.py:41
  165.7 0.7 copy.27
  166.4 3.4 all-to-all-start.3
  169.8 0.6 dynamic-slice_reduce_fusion.1
  171.6 7.0 %all-to-all-done.3 = f32[4,8,16,128]{3,2,0,1:T(8,128)S(1)} async-done(((f32[4,8,16,128]{3,2,0,1:T(8,128)}), f32[4,8,16,128]{3,2,0,1:T(8,128)S(1)}, u32[]{:S(2)}, u32[]{:S(2)}) %all-to-all-start.3) | async-done | bytes 262176 | tf_op jit(solution)/shard_map/all_to_all | solution.py:40
  178.6 0.6 multiply_reduce_fusion.1
  179.2 38.9 %all-reduce.1 = (f32[]{:T(128)}, f32[]{:T(128)}) all-reduce(f32[]{:T(128)S(6)} %add.100, f32[]{:T(128)} %multiply_reduce_fusion.1), channel_id=1, replica_groups=mesh['narrow'=4,'wide'=8] {'narrow','wide'}, use_global_device_ids=true, to_apply=%region_8.10 | all-reduce | flops 2 | bytes 16 | tf_op jit(solution)/shard_map/psum | solution.py:50
  219.5 67.5 %all_gather.10 = f32[512,128]{1,0:T(8,128)S(1)} all-gather(f32[16,128]{1,0:T(8,128)S(1)} %add_maximum_fusion.1), channel_id=1, replica_groups=mesh['narrow'=4,'wide'=8] {'narrow','wide'}, dimensions={0}, use_global_device_ids=true | all-gather | bytes 270336 | tf_op jit(solution)/shard_map/all_gather | solution.py:56
  286.9 0.6 gather_fusion.2
  287.6 4.1 fusion.2
  291.8 0.6 fusion.29
  292.4 3.4 fusion
  295.8 0.3 fusion.12
  296.1 8.4 %all_to_all.32 = f32[4,8,16,128]{3,2,1,0:T(8,128)S(1)} all-to-all(f32[4,8,16,128]{3,2,1,0:T(8,128)S(1)} %fusion.12), channel_id=1, replica_groups=mesh['narrow'=4,'wide'=8] {'narrow'}, dimensions={0} | all-to-all | bytes 524288 | tf_op jit(solution)/shard_map/all_to_all | solution.py:41
  304.5 0.7 copy.30
  305.2 3.4 all-to-all-start.5
  308.7 0.6 dynamic-slice_reduce_fusion
  310.5 6.9 %all-to-all-done.5 = f32[4,8,16,128]{3,2,0,1:T(8,128)S(1)} async-done(((f32[4,8,16,128]{3,2,0,1:T(8,128)}), f32[4,8,16,128]{3,2,0,1:T(8,128)S(1)}, u32[]{:S(2)}, u32[]{:S(2)}) %all-to-all-start.5) | async-done | bytes 262176 | tf_op jit(solution)/shard_map/all_to_all | solution.py:40
  317.5 0.6 multiply_reduce_fusion
  318.1 38.9 %all-reduce = (f32[]{:T(128)}, f32[]{:T(128)}) all-reduce(f32[]{:T(128)S(6)} %add.106, f32[]{:T(128)} %multiply_reduce_fusion), channel_id=1, replica_groups=mesh['narrow'=4,'wide'=8] {'narrow','wide'}, use_global_device_ids=true, to_apply=%region_15.17 | all-reduce | flops 2 | bytes 16 | tf_op jit(solution)/shard_map/psum | solution.py:50
  358.2 67.3 %all_gather.11 = f32[512,128]{1,0:T(8,128)S(1)} all-gather(f32[16,128]{1,0:T(8,128)S(1)} %add_maximum_fusion), channel_id=1, replica_groups=mesh['narrow'=4,'wide'=8] {'narrow','wide'}, dimensions={0}, use_global_device_ids=true | all-gather | bytes 270336 | tf_op jit(solution)/shard_map/all_gather | solution.py:56
  425.5 0.7 copy.48
  (20 shorter events, 0.4 us)
Async XLA Ops:
  0.6 8.3 %copy-start.3 = (s32[16,128]{1,0:T(8,128)S(1)}, s32[16,128]{1,0:T(8,128)}, u32[]{:S(2)}) copy-start(s32[16,128]{1,0:T(8,128)} %param.9) | copy-start | bytes 24580
  4.7 4.9 %copy-start = (s32[16,4,128,128]{3,2,1,0:T(8,128)S(1)}, s32[16,4,128,128]{3,2,1,0:T(8,128)}, u32[]{:S(2)}) copy-start(s32[16,4,128,128]{3,2,1,0:T(8,128)} %param.8) | copy-start | bytes 12582916
  24.1 14.4 %all-to-all-start.1 = ((f32[4,8,16,128]{3,2,0,1:T(8,128)}), f32[4,8,16,128]{3,2,0,1:T(8,128)S(1)}, u32[]{:S(2)}, u32[]{:S(2)}) async-start(f32[4,8,16,128]{3,2,0,1:T(8,128)} %copy.24), calls=%async_computation.1 | async-start | bytes 524288 | tf_op jit(solution)/shard_map/all_to_all | solution.py:40
  148.7 4.8 %copy-start.1 = (s32[16,4,128,128]{3,2,1,0:T(8,128)S(1)}, s32[16,4,128,128]{3,2,1,0:T(8,128)}, u32[]{:S(2)}) copy-start(s32[16,4,128,128]{3,2,1,0:T(8,128)} %param.8) | copy-start | bytes 12582916
  166.4 12.2 %all-to-all-start.3 = ((f32[4,8,16,128]{3,2,0,1:T(8,128)}), f32[4,8,16,128]{3,2,0,1:T(8,128)S(1)}, u32[]{:S(2)}, u32[]{:S(2)}) async-start(f32[4,8,16,128]{3,2,0,1:T(8,128)} %copy.27), calls=%async_computation.3 | async-start | bytes 524288 | tf_op jit(solution)/shard_map/all_to_all | solution.py:40
  287.5 4.8 %copy-start.2 = (s32[16,4,128,128]{3,2,1,0:T(8,128)S(1)}, s32[16,4,128,128]{3,2,1,0:T(8,128)}, u32[]{:S(2)}) copy-start(s32[16,4,128,128]{3,2,1,0:T(8,128)} %param.8) | copy-start | bytes 12582916
  292.4 133.9 %copy-start.4 = (f32[16,128]{1,0:T(8,128)}, f32[16,128]{1,0:T(8,128)S(1)}, u32[]{:S(2)}) copy-start(f32[16,128]{1,0:T(8,128)S(1)} %get-tuple-element.18) | copy-start | bytes 24580
  305.2 12.2 %all-to-all-start.5 = ((f32[4,8,16,128]{3,2,0,1:T(8,128)}), f32[4,8,16,128]{3,2,0,1:T(8,128)S(1)}, u32[]{:S(2)}, u32[]{:S(2)}) async-start(f32[4,8,16,128]{3,2,0,1:T(8,128)} %copy.30), calls=%async_computation.5 | async-start | bytes 524288 | tf_op jit(solution)/shard_map/all_to_all | solution.py:40
where the time goes:
time: 427 us; the launch traced here: 426 us
  blocking collectives  346 us (81%)
  matrix products  23.5 us (6%)
  waiting for transfers between devices  19.7 us (5%)
  starting transfers between devices  12.7 us (3%)
  between operations  9.14 us (2%)
  other arithmetic  8.77 us (2%)
  local copies, waits for them, and re-layouts  6.74 us (2%)
    all_gather x3, blocking collectives, local(): mult = lax.all_gather(new_share, ('narrow', 'wide'), axis=0, tiled=True)  202 us
    psum x3, blocking collectives, local(): lax.psum((jnp.sum(slope * slope), jnp.sum(mult_share), local_soft), ('nar...  117 us
    all_to_all x3, blocking collectives, local(): lax.all_to_all(outgoing, 'narrow', split_axis=0, concat_axis=0, tiled=True)  26.8 us
    all_to_all x3, waiting for transfers between devices, local(): lax.all_to_all(lax.all_to_all(outgoing, 'narrow', split_axis=0, concat_ax...  19.7 us
    all_to_all x3, starting transfers between devices, local(): lax.all_to_all(lax.all_to_all(outgoing, 'narrow', split_axis=0, concat_ax...  12.7 us
    dot_general x3, matrix products, local(): reduced = costf - jnp.einsum('tkrc,tkr->tc', incf, u_tile, precision=hi)  12.3 us
    dot_general x3, matrix products, local(): jnp.einsum('tkrc,tc->tkr', incf, primal_mean, precision=hi)  10.2 us
  transfers between devices with their start and end apart: 3, of which 3 were waited for; matrix products, arithmetic and copies ran while one was open for 1% of the time, Pallas kernels for 0%

commit v1 on v0

--- a/solution.py
+++ b/solution.py
@@ -48,7 +48,7 @@
         mult_share = lax.dynamic_slice_in_dim(mult, share_start, share_rows, 0)
         slope = 1.0 - cover_share
         norm, mult_total, late_sum = lax.psum(
-            (jnp.sum(slope * slope), jnp.sum(mult_share), local_soft), ("narrow", "wide")
+            lax.psum((jnp.sum(slope * slope), jnp.sum(mult_share), local_soft), "wide"), "narrow"
         )
         value = mult_total + late_sum
         size = (upper[0] - value) / (norm + 1e-06)

time: 427 us -> 382 us (0.89)
  blocking collectives: 346 us -> 300 us
    psum x3 -> x6, blocking collectives: 117 us -> 79 us  [the longest x3 60.2 us: local(): lax.psum((jnp.sum(slope * slope), jnp.sum(mult_share), local_soft), 'wide')]
    all_gather x3, blocking collectives: 202 us -> 194 us  [local(): mult = lax.all_gather(new_share, ('narrow', 'wide'), axis=0, tiled=True)]
where the time goes in v1:
time: 382 us; the launch traced here: 381 us
  blocking collectives  300 us (79%)
  matrix products  23.5 us (6%)
  waiting for transfers between devices  19.5 us (5%)
  starting transfers between devices  13 us (3%)
  between operations  9.12 us (2%)
  other arithmetic  8.75 us (2%)
  local copies, waits for them, and re-layouts  6.74 us (2%)
    all_gather x3, blocking collectives, local(): mult = lax.all_gather(new_share, ('narrow', 'wide'), axis=0, tiled=True)  194 us
    psum x3, blocking collectives, local(): lax.psum((jnp.sum(slope * slope), jnp.sum(mult_share), local_soft), 'wide')  60.2 us
    all_to_all x3, blocking collectives, local(): lax.all_to_all(outgoing, 'narrow', split_axis=0, concat_axis=0, tiled=True)  26.8 us
    all_to_all x3, waiting for transfers between devices, local(): lax.all_to_all(lax.all_to_all(outgoing, 'narrow', split_axis=0, concat_ax...  19.5 us
    psum x3, blocking collectives, local(): lax.psum(lax.psum((jnp.sum(slope * slope), jnp.sum(mult_share), local_sof...  18.8 us
    all_to_all x3, starting transfers between devices, local(): lax.all_to_all(lax.all_to_all(outgoing, 'narrow', split_axis=0, concat_ax...  13 us
    dot_general x3, matrix products, local(): reduced = costf - jnp.einsum('tkrc,tkr->tc', incf, u_tile, precision=hi)  12.3 us
    dot_general x3, matrix products, local(): jnp.einsum('tkrc,tc->tkr', incf, primal_mean, precision=hi)  10.2 us
  transfers between devices with their start and end apart: 3, of which 3 were waited for; matrix products, arithmetic and copies ran while one was open for 1% of the time, Pallas kernels for 0%

profile of v1, /device:TPU:0, one launch (start us, length us, event | category | flops | bytes accessed | tf_op | source)
XLA Modules:
  0.0 380.7 jit_solution(17048576300980439168)
XLA Ops:
  0.6 0.7 compare_and_fusion
  1.3 0.7 compare_select_fusion.3
  2.0 0.8 copy.23
  2.8 0.1 copy.21
  3.2 1.5 gather_fusion
  4.8 4.1 %fusion.10 = f32[16,1,128,1]{2,1,3,0:T(1,128)S(1)} fusion(f32[16,4,128,1]{2,3,1,0:T(1,128)S(1)} %bitcast.71, s32[16,4,128,128]{3,2,1,0:T(8,128)} %param.8), kind=kOutput, calls=%fused_computation.13 | convolution fusion | flops 13631488 | bytes 4235264 | tf_op jit(solution)/shard_map/tkrc,tkr->tc/dot_general | solution.py:28
  8.9 0.6 fusion.25
  9.6 3.4 fusion.8
  12.9 0.3 fusion.16
  13.3 10.0 %all_to_all.30 = f32[4,8,16,128]{3,2,1,0:T(8,128)S(1)} all-to-all(f32[4,8,16,128]{3,2,1,0:T(8,128)S(1)} %fusion.16), channel_id=1, replica_groups=mesh['narrow'=4,'wide'=8] {'narrow'}, dimensions={0} | all-to-all | bytes 524288 | tf_op jit(solution)/shard_map/all_to_all | solution.py:41
  23.3 0.7 copy.24
  24.1 5.8 %all-to-all-start.1 = ((f32[4,8,16,128]{3,2,0,1:T(8,128)}), f32[4,8,16,128]{3,2,0,1:T(8,128)S(1)}, u32[]{:S(2)}, u32[]{:S(2)}) async-start(f32[4,8,16,128]{3,2,0,1:T(8,128)} %copy.24), calls=%async_computation.1 | async-start | bytes 524288 | tf_op jit(solution)/shard_map/all_to_all | solution.py:40
  29.9 1.4 dynamic-slice_reduce_fusion.2
  32.6 5.8 %all-to-all-done.1 = f32[4,8,16,128]{3,2,0,1:T(8,128)S(1)} async-done(((f32[4,8,16,128]{3,2,0,1:T(8,128)}), f32[4,8,16,128]{3,2,0,1:T(8,128)S(1)}, u32[]{:S(2)}, u32[]{:S(2)}) %all-to-all-start.1) | async-done | bytes 262176 | tf_op jit(solution)/shard_map/all_to_all | solution.py:40
  38.5 0.6 multiply_reduce_fusion.2
  39.7 20.1 %all-reduce.2 = (f32[]{:T(128)}, f32[]{:T(128)}) all-reduce(f32[]{:T(128)S(6)} %add.113, f32[]{:T(128)} %multiply_reduce_fusion.2), channel_id=1, replica_groups=mesh['narrow'=4,'wide'=8] {'wide'}, use_global_device_ids=true, to_apply=%region_1.2 | all-reduce | flops 2 | bytes 16 | tf_op jit(solution)/shard_map/psum | solution.py:51
  59.8 6.3 %all-reduce.5 = (f32[]{:T(128)}, f32[]{:T(128)}) all-reduce(f32[]{:T(128)} %get-tuple-element.7, f32[]{:T(128)} %get-tuple-element.8), channel_id=1, replica_groups=mesh['narrow'=4,'wide'=8] {'narrow'}, use_global_device_ids=true, to_apply=%region_2.3 | all-reduce | flops 2 | bytes 16 | tf_op jit(solution)/shard_map/psum | solution.py:50
  67.4 0.7 add_maximum_fusion.2
  68.1 64.7 %all_gather.9 = f32[512,128]{1,0:T(8,128)S(1)} all-gather(f32[16,128]{1,0:T(8,128)S(1)} %add_maximum_fusion.2), channel_id=1, replica_groups=mesh['narrow'=4,'wide'=8] {'narrow','wide'}, dimensions={0}, use_global_device_ids=true | all-gather | bytes 270336 | tf_op jit(solution)/shard_map/all_gather | solution.py:56
  132.8 0.6 gather_fusion.1
  133.5 4.1 %fusion.6 = f32[16,1,128,1]{2,1,3,0:T(1,128)S(1)} fusion(f32[16,4,128,1]{2,3,1,0:T(1,128)S(1)} %bitcast.72, s32[16,4,128,128]{3,2,1,0:T(8,128)} %param.8), kind=kOutput, calls=%fused_computation.9 | convolution fusion | flops 13631488 | bytes 4235264 | tf_op jit(solution)/shard_map/tkrc,tkr->tc/dot_general | solution.py:28
  137.7 0.6 fusion.27
  138.3 3.4 fusion.4
  141.7 0.3 fusion.14
  142.0 8.4 %all_to_all.31 = f32[4,8,16,128]{3,2,1,0:T(8,128)S(1)} all-to-all(f32[4,8,16,128]{3,2,1,0:T(8,128)S(1)} %fusion.14), channel_id=1, replica_groups=mesh['narrow'=4,'wide'=8] {'narrow'}, dimensions={0} | all-to-all | bytes 524288 | tf_op jit(solution)/shard_map/all_to_all | solution.py:41
  150.4 0.7 copy.27
  151.1 3.6 all-to-all-start.3
  154.7 0.6 dynamic-slice_reduce_fusion.1
  156.5 6.8 %all-to-all-done.3 = f32[4,8,16,128]{3,2,0,1:T(8,128)S(1)} async-done(((f32[4,8,16,128]{3,2,0,1:T(8,128)}), f32[4,8,16,128]{3,2,0,1:T(8,128)S(1)}, u32[]{:S(2)}, u32[]{:S(2)}) %all-to-all-start.3) | async-done | bytes 262176 | tf_op jit(solution)/shard_map/all_to_all | solution.py:40
  163.4 0.6 multiply_reduce_fusion.1
  164.0 20.1 %all-reduce.1 = (f32[]{:T(128)}, f32[]{:T(128)}) all-reduce(f32[]{:T(128)S(6)} %add.118, f32[]{:T(128)} %multiply_reduce_fusion.1), channel_id=1, replica_groups=mesh['narrow'=4,'wide'=8] {'wide'}, use_global_device_ids=true, to_apply=%region_11.13 | all-reduce | flops 2 | bytes 16 | tf_op jit(solution)/shard_map/psum | solution.py:51
  184.0 6.3 %all-reduce.4 = (f32[]{:T(128)}, f32[]{:T(128)}) all-reduce(f32[]{:T(128)} %get-tuple-element.5, f32[]{:T(128)} %get-tuple-element.6), channel_id=1, replica_groups=mesh['narrow'=4,'wide'=8] {'narrow'}, use_global_device_ids=true, to_apply=%region_12.14 | all-reduce | flops 2 | bytes 16 | tf_op jit(solution)/shard_map/psum | solution.py:50
  191.7 64.9 %all_gather.10 = f32[512,128]{1,0:T(8,128)S(1)} all-gather(f32[16,128]{1,0:T(8,128)S(1)} %add_maximum_fusion.1), channel_id=1, replica_groups=mesh['narrow'=4,'wide'=8] {'narrow','wide'}, dimensions={0}, use_global_device_ids=true | all-gather | bytes 270336 | tf_op jit(solution)/shard_map/all_gather | solution.py:56
  256.6 0.6 gather_fusion.2
  257.2 4.1 %fusion.2 = f32[16,1,128,1]{2,1,3,0:T(1,128)S(1)} fusion(f32[16,4,128,1]{2,3,1,0:T(1,128)S(1)} %bitcast.70, s32[16,4,128,128]{3,2,1,0:T(8,128)} %param.8), kind=kOutput, calls=%fused_computation.5 | convolution fusion | flops 13631488 | bytes 4235264 | tf_op jit(solution)/shard_map/tkrc,tkr->tc/dot_general | solution.py:28
  261.4 0.6 fusion.29
  262.0 3.4 fusion
  265.4 0.3 fusion.12
  265.7 8.4 %all_to_all.32 = f32[4,8,16,128]{3,2,1,0:T(8,128)S(1)} all-to-all(f32[4,8,16,128]{3,2,1,0:T(8,128)S(1)} %fusion.12), channel_id=1, replica_groups=mesh['narrow'=4,'wide'=8] {'narrow'}, dimensions={0} | all-to-all | bytes 524288 | tf_op jit(solution)/shard_map/all_to_all | solution.py:41
  274.1 0.7 copy.30
  274.8 3.6 all-to-all-start.5
  278.4 0.6 dynamic-slice_reduce_fusion
  280.2 6.8 %all-to-all-done.5 = f32[4,8,16,128]{3,2,0,1:T(8,128)S(1)} async-done(((f32[4,8,16,128]{3,2,0,1:T(8,128)}), f32[4,8,16,128]{3,2,0,1:T(8,128)S(1)}, u32[]{:S(2)}, u32[]{:S(2)}) %all-to-all-start.5) | async-done | bytes 262176 | tf_op jit(solution)/shard_map/all_to_all | solution.py:40
  287.1 0.6 multiply_reduce_fusion
  287.7 20.1 %all-reduce = (f32[]{:T(128)}, f32[]{:T(128)}) all-reduce(f32[]{:T(128)S(6)} %add.124, f32[]{:T(128)} %multiply_reduce_fusion), channel_id=1, replica_groups=mesh['narrow'=4,'wide'=8] {'wide'}, use_global_device_ids=true, to_apply=%region_21.23 | all-reduce | flops 2 | bytes 16 | tf_op jit(solution)/shard_map/psum | solution.py:51
  307.8 6.3 %all-reduce.3 = (f32[]{:T(128)}, f32[]{:T(128)}) all-reduce(f32[]{:T(128)} %get-tuple-element.3, f32[]{:T(128)} %get-tuple-element.4), channel_id=1, replica_groups=mesh['narrow'=4,'wide'=8] {'narrow'}, use_global_device_ids=true, to_apply=%region_22.24 | all-reduce | flops 2 | bytes 16 | tf_op jit(solution)/shard_map/psum | solution.py:50
  315.3 64.7 %all_gather.11 = f32[512,128]{1,0:T(8,128)S(1)} all-gather(f32[16,128]{1,0:T(8,128)S(1)} %add_maximum_fusion), channel_id=1, replica_groups=mesh['narrow'=4,'wide'=8] {'narrow','wide'}, dimensions={0}, use_global_device_ids=true | all-gather | bytes 270336 | tf_op jit(solution)/shard_map/all_gather | solution.py:56
  380.0 0.7 copy.48
  (23 shorter events, 0.7 us)
Async XLA Ops:
  0.6 8.3 %copy-start.3 = (s32[16,128]{1,0:T(8,128)S(1)}, s32[16,128]{1,0:T(8,128)}, u32[]{:S(2)}) copy-start(s32[16,128]{1,0:T(8,128)} %param.9) | copy-start | bytes 24580
  4.7 4.9 %copy-start = (s32[16,4,128,128]{3,2,1,0:T(8,128)S(1)}, s32[16,4,128,128]{3,2,1,0:T(8,128)}, u32[]{:S(2)}) copy-start(s32[16,4,128,128]{3,2,1,0:T(8,128)} %param.8) | copy-start | bytes 12582916
  24.1 14.4 %all-to-all-start.1 = ((f32[4,8,16,128]{3,2,0,1:T(8,128)}), f32[4,8,16,128]{3,2,0,1:T(8,128)S(1)}, u32[]{:S(2)}, u32[]{:S(2)}) async-start(f32[4,8,16,128]{3,2,0,1:T(8,128)} %copy.24), calls=%async_computation.1 | async-start | bytes 524288 | tf_op jit(solution)/shard_map/all_to_all | solution.py:40
  133.4 4.8 %copy-start.1 = (s32[16,4,128,128]{3,2,1,0:T(8,128)S(1)}, s32[16,4,128,128]{3,2,1,0:T(8,128)}, u32[]{:S(2)}) copy-start(s32[16,4,128,128]{3,2,1,0:T(8,128)} %param.8) | copy-start | bytes 12582916
  151.1 12.2 %all-to-all-start.3 = ((f32[4,8,16,128]{3,2,0,1:T(8,128)}), f32[4,8,16,128]{3,2,0,1:T(8,128)S(1)}, u32[]{:S(2)}, u32[]{:S(2)}) async-start(f32[4,8,16,128]{3,2,0,1:T(8,128)} %copy.27), calls=%async_computation.3 | async-start | bytes 524288 | tf_op jit(solution)/shard_map/all_to_all | solution.py:40
  257.2 4.8 %copy-start.2 = (s32[16,4,128,128]{3,2,1,0:T(8,128)S(1)}, s32[16,4,128,128]{3,2,1,0:T(8,128)}, u32[]{:S(2)}) copy-start(s32[16,4,128,128]{3,2,1,0:T(8,128)} %param.8) | copy-start | bytes 12582916
  262.0 118.7 %copy-start.4 = (f32[16,128]{1,0:T(8,128)}, f32[16,128]{1,0:T(8,128)S(1)}, u32[]{:S(2)}) copy-start(f32[16,128]{1,0:T(8,128)S(1)} %get-tuple-element.24) | copy-start | bytes 24580
  274.8 12.2 %all-to-all-start.5 = ((f32[4,8,16,128]{3,2,0,1:T(8,128)}), f32[4,8,16,128]{3,2,0,1:T(8,128)S(1)}, u32[]{:S(2)}, u32[]{:S(2)}) async-start(f32[4,8,16,128]{3,2,0,1:T(8,128)} %copy.30), calls=%async_computation.5 | async-start | bytes 524288 | tf_op jit(solution)/shard_map/all_to_all | solution.py:40
